TPU v7x, 32 devices: a whole 2x2x4 slice. The times are simulated.
32 devices in a mesh: gx: 8 (over z, y), gy: 4 (over x, core).
Axes of the slice: x: 2, y: 2, z: 4, core: 2. Of those that a mesh axis runs over, the one named last changes fastest.
Arguments:
- anomalies: float32 [80, 16, 32, 128], P(None, 'gx', 'gy'), may hold values from -6 to 6
- state_mean: float32 [16, 32, 128], P('gx', 'gy'), may hold values from -6 to 6
- obs_value: float32 [16, 256], P(None, 'gy'), may hold values from -8 to 8
- obs_cell: int32 [16, 256], replicated, may hold values from 0 to 2047
- owner: int32 [16], replicated, may hold values from 0 to 7, as said below
- order: int32 [16], replicated, may hold values from 0 to 15, each once
- root_inv: float32 [16, 256, 256], P(None, 'gy'), as said below
- gain_inv: float32 [16, 256, 256], P(None, 'gy'), as said below
Outputs:
- post_anomalies: float32 [80, 16, 32, 128], P(None, 'gx', 'gy')
- post_mean: float32 [16, 32, 128], P('gx', 'gy')
Inputs may be any that keep to these rules, and one draw needn't show every extreme that they name: `owner`: some batch lies at slab 8 - 2, some at slab 1 and some at slab 8 // 2; the others favour low slabs. `order`: each batch number once. `root_inv`: symmetric. `gain_inv`: symmetric.
All inputs are finite; a program needn't handle non-finite values.
Results may differ from a plain program's by a relative error of at most 0.0001.
Values sent between devices are 32-bit elements; how exact they have to be, the bound alone decides.
A program may use at most 64 MiB of HBM per device.

v0:
```python
import jax
import jax.numpy as jnp
from jax import lax
from jax.sharding import PartitionSpec as P

BATCHES = 16
REACH = 3


def shifted(value, axis, steps):
    count = lax.axis_size(axis)
    pairs = [(source, (source + steps) % count) for source in range(count)]
    return lax.ppermute(value, axis, pairs)


def product(left_side, right_side):
    return jnp.dot(
        left_side, right_side, precision=lax.Precision.HIGHEST, preferred_element_type=jnp.float32
    )


def prior_direct(masked):
    total = masked
    for step in range(1, REACH + 1):
        for sign_step in [step, -step]:
            total = total + shifted(masked, "gx", sign_step)
    return total


def local(anomalies, state_mean, obs_value, obs_cell, owner, order, root_inv, gain_inv):
    members, lon_dev, lat_dev, levels = anomalies.shape
    cell_count = lon_dev * lat_dev * levels
    quarter = obs_value.shape[1]
    obs_total = obs_cell.shape[1]
    slab_count = lax.axis_size("gx")
    band_count = lax.axis_size("gy")
    column = lax.axis_index("gx")
    band_index = lax.axis_index("gy")
    lon_total = slab_count * lon_dev
    lat_total = band_count * lat_dev
    taper_span = REACH * lon_dev + 1.0
    cell_ids = jnp.arange(cell_count, dtype=jnp.int32)
    cell_lon = column * lon_dev + cell_ids // (lat_dev * levels)
    cell_lat = band_index * lat_dev + cell_ids // levels % lat_dev
    obs_band = jnp.arange(obs_total, dtype=jnp.int32) // quarter

    def assimilate(batch_turn, carried):
        state_rows, mean_row = carried
        batch_id = order[batch_turn]
        root_slab = owner[batch_id]
        is_root = column == root_slab
        cells_of = obs_cell[batch_id]
        local_ids = lax.dynamic_slice_in_dim(cells_of, band_index * quarter, quarter)
        picked = jnp.take(state_rows, local_ids, axis=1)
        innovation = obs_value[batch_id] - jnp.take(mean_row, local_ids)
        root_rows = root_inv[batch_id]
        gain_rows = gain_inv[batch_id]
        joined = jnp.concatenate([picked, innovation[None, :]], axis=0)
        masked = jnp.where(is_root, joined, jnp.zeros_like(joined))
        joined = prior_direct(masked)
        picked, innovation = (joined[:members], joined[members])
        prior_all, innov_all = (
            lax.all_gather(picked, "gy", axis=1, tiled=True),
            lax.all_gather(innovation, "gy", axis=0, tiled=True),
        )
        weighted = product(prior_all, root_rows.T)
        gain_part = product(gain_rows, innov_all)
        weighted_all, gain_all = (
            lax.all_gather(weighted, "gy", axis=1, tiled=True),
            lax.all_gather(gain_part, "gy", axis=0, tiled=True),
        )
        obs_lon = root_slab * lon_dev + cells_of // (lat_dev * levels)
        obs_lat = obs_band * lat_dev + cells_of // levels % lat_dev
        slab_gap = jnp.abs(column - root_slab)
        in_reach = jnp.minimum(slab_gap, slab_count - slab_gap) <= REACH

        def near_update(operands):
            rows_now, mean_now = operands
            lon_gap = jnp.abs(obs_lon[:, None] - cell_lon[None, :])
            cycle_gap = jnp.minimum(lon_gap, lon_total - lon_gap)
            lat_gap = jnp.abs(obs_lat[:, None] - cell_lat[None, :])
            taper_rows = jnp.maximum(0.0, 1.0 - cycle_gap.astype(jnp.float32) / taper_span) * (
                1.0 - lat_gap.astype(jnp.float32) / lat_total
            )
            covariance = product(prior_all.T, rows_now) / (members - 1.0)
            gained = taper_rows * covariance
            stacked = jnp.concatenate([weighted_all, gain_all[None, :]], axis=0)
            increment = product(stacked, gained)
            return (rows_now - increment[:members], mean_now + increment[members])

        def keep_all(operands):
            return operands

        return lax.cond(in_reach, near_update, keep_all, (state_rows, mean_row))

    start_rows = anomalies.reshape(members, cell_count)
    start_mean = state_mean.reshape(cell_count)
    final_rows, final_mean = lax.fori_loop(0, BATCHES, assimilate, (start_rows, start_mean))
    return (
        final_rows.reshape(members, lon_dev, lat_dev, levels),
        final_mean.reshape(lon_dev, lat_dev, levels),
    )


def solution(mesh):
    return jax.shard_map(
        local,
        mesh=mesh,
        in_specs=(
            P(None, "gx", "gy", None),
            P("gx", "gy", None),
            P(None, "gy"),
            P(),
            P(),
            P(),
            P(None, "gy", None),
            P(None, "gy", None),
        ),
        out_specs=(P(None, "gx", "gy", None), P("gx", "gy", None)),
        check_vma=False,
    )
```

profile of v0, /device:TPU:0, one launch (start us, length us, event | category | flops | bytes accessed | tf_op | source)
XLA Modules:
  0.0 857.3 jit_solution(17424836850244703015)
XLA Ops:
  3.4 852.9 %while.19 = (s32[]{:T(128)}, f32[80,2048]{1,0:T(8,128)S(1)}, f32[2048]{0:T(1024)S(1)}, s32[16]{0:T(128)}, s32[16]{0:T(128)}, /*index=5*/s32[]{:T(128)}, s32[16,2...) while((s32[]{:T(128)}, f32[80,2048]{1,0:T(8,128)S(1)}, ...), condition=%wide.region_3.4_spmd.clone, body=%wide.region_0.3_spmd.clone.sunk | while | flops 1037555904 | bytes 10573724 | solution.py:98
  27.9 5.6 all-reduce.6
  34.7 6.7 all-reduce.7
  81.8 5.6 all-reduce.6
  88.7 6.1 all-reduce.7
  132.2 5.6 all-reduce.6
  139.1 6.6 all-reduce.7
  186.0 5.6 all-reduce.6
  192.9 6.1 all-reduce.7
  239.4 5.6 all-reduce.6
  246.2 6.6 all-reduce.7
  293.2 5.6 all-reduce.6
  300.0 6.1 all-reduce.7
  346.5 5.6 all-reduce.6
  353.4 6.6 all-reduce.7
  400.3 5.6 all-reduce.6
  407.2 6.1 all-reduce.7
  453.7 5.6 all-reduce.6
  460.5 6.6 all-reduce.7
  507.5 5.6 all-reduce.6
  514.3 6.1 all-reduce.7
  560.8 5.6 all-reduce.6
  567.7 6.6 all-reduce.7
  614.7 5.6 all-reduce.6
  621.5 6.1 all-reduce.7
  668.0 5.6 all-reduce.6
  674.8 6.6 all-reduce.7
  721.8 5.6 all-reduce.6
  728.7 6.1 all-reduce.7
  772.2 5.6 all-reduce.6
  779.1 6.6 all-reduce.7
  832.9 6.1 all-reduce.7
  (919 shorter events, 675.6 us)
Async XLA Ops:
  11.5 9.9 %collective-permute-start.5 = (f32[81,64]{0,1:T(8,128)S(1)}, f32[81,64]{0,1:T(8,128)S(1)}, u32[]{:S(2)}, u32[]{:S(2)}) collective-permute-start(f32[81,64]{0,1:T(8,128)S(1)} %maximum_select_fusion.2), channel_id=1, source_target_pairs={{0,4},{4,8},{8,12},{12,16},{16,20},{20,24},{24,28},{28,0},{1,5},{5... | collective-permute-start | bytes 62216 | tf_op jit(solution)/shard_map/while/body/eval_jaxpr/ppermute | solution.py:13
  14.5 12.8 %collective-permute-start.4 = (f32[81,64]{0,1:T(8,128)S(1)}, f32[81,64]{0,1:T(8,128)S(1)}, u32[]{:S(2)}, u32[]{:S(2)}) collective-permute-start(f32[81,64]{0,1:T(8,128)S(1)} %maximum_select_fusion.2), channel_id=1, source_target_pairs={{0,28},{4,0},{8,4},{12,8},{16,12},{20,16},{24,20},{28,24},{1,29},{... | collective-permute-start | bytes 62216 | tf_op jit(solution)/shard_map/while/body/eval_jaxpr/ppermute | solution.py:13
  17.6 9.7 %collective-permute-start.2 = (f32[81,64]{0,1:T(8,128)S(1)}, f32[81,64]{0,1:T(8,128)S(1)}, u32[]{:S(2)}, u32[]{:S(2)}) collective-permute-start(f32[81,64]{0,1:T(8,128)S(1)} %maximum_select_fusion.2), channel_id=1, source_target_pairs={{0,24},{4,28},{8,0},{12,4},{16,8},{20,12},{24,16},{28,20},{1,25},{... | collective-permute-start | bytes 62216 | tf_op jit(solution)/shard_map/while/body/eval_jaxpr/ppermute | solution.py:13
  67.2 14.1 %collective-permute-start.4 = (f32[81,64]{0,1:T(8,128)S(1)}, f32[81,64]{0,1:T(8,128)S(1)}, u32[]{:S(2)}, u32[]{:S(2)}) collective-permute-start(f32[81,64]{0,1:T(8,128)S(1)} %maximum_select_fusion.2), channel_id=1, source_target_pairs={{0,28},{4,0},{8,4},{12,8},{16,12},{20,16},{24,20},{28,24},{1,29},{... | collective-permute-start | bytes 62216 | tf_op jit(solution)/shard_map/while/body/eval_jaxpr/ppermute | solution.py:13
  71.6 9.7 %collective-permute-start.2 = (f32[81,64]{0,1:T(8,128)S(1)}, f32[81,64]{0,1:T(8,128)S(1)}, u32[]{:S(2)}, u32[]{:S(2)}) collective-permute-start(f32[81,64]{0,1:T(8,128)S(1)} %maximum_select_fusion.2), channel_id=1, source_target_pairs={{0,24},{4,28},{8,0},{12,4},{16,8},{20,12},{24,16},{28,20},{1,25},{... | collective-permute-start | bytes 62216 | tf_op jit(solution)/shard_map/while/body/eval_jaxpr/ppermute | solution.py:13
  114.8 11.7 %collective-permute-start.5 = (f32[81,64]{0,1:T(8,128)S(1)}, f32[81,64]{0,1:T(8,128)S(1)}, u32[]{:S(2)}, u32[]{:S(2)}) collective-permute-start(f32[81,64]{0,1:T(8,128)S(1)} %maximum_select_fusion.2), channel_id=1, source_target_pairs={{0,4},{4,8},{8,12},{12,16},{16,20},{20,24},{24,28},{28,0},{1,5},{5... | collective-permute-start | bytes 62216 | tf_op jit(solution)/shard_map/while/body/eval_jaxpr/ppermute | solution.py:13
  119.2 12.0 %collective-permute-start.4 = (f32[81,64]{0,1:T(8,128)S(1)}, f32[81,64]{0,1:T(8,128)S(1)}, u32[]{:S(2)}, u32[]{:S(2)}) collective-permute-start(f32[81,64]{0,1:T(8,128)S(1)} %maximum_select_fusion.2), channel_id=1, source_target_pairs={{0,28},{4,0},{8,4},{12,8},{16,12},{20,16},{24,20},{28,24},{1,29},{... | collective-permute-start | bytes 62216 | tf_op jit(solution)/shard_map/while/body/eval_jaxpr/ppermute | solution.py:13
  173.1 12.4 %collective-permute-start.4 = (f32[81,64]{0,1:T(8,128)S(1)}, f32[81,64]{0,1:T(8,128)S(1)}, u32[]{:S(2)}, u32[]{:S(2)}) collective-permute-start(f32[81,64]{0,1:T(8,128)S(1)} %maximum_select_fusion.2), channel_id=1, source_target_pairs={{0,28},{4,0},{8,4},{12,8},{16,12},{20,16},{24,20},{28,24},{1,29},{... | collective-permute-start | bytes 62216 | tf_op jit(solution)/shard_map/while/body/eval_jaxpr/ppermute | solution.py:13
  175.8 9.7 %collective-permute-start.2 = (f32[81,64]{0,1:T(8,128)S(1)}, f32[81,64]{0,1:T(8,128)S(1)}, u32[]{:S(2)}, u32[]{:S(2)}) collective-permute-start(f32[81,64]{0,1:T(8,128)S(1)} %maximum_select_fusion.2), channel_id=1, source_target_pairs={{0,24},{4,28},{8,0},{12,4},{16,8},{20,12},{24,16},{28,20},{1,25},{... | collective-permute-start | bytes 62216 | tf_op jit(solution)/shard_map/while/body/eval_jaxpr/ppermute | solution.py:13
  224.6 14.2 %collective-permute-start.4 = (f32[81,64]{0,1:T(8,128)S(1)}, f32[81,64]{0,1:T(8,128)S(1)}, u32[]{:S(2)}, u32[]{:S(2)}) collective-permute-start(f32[81,64]{0,1:T(8,128)S(1)} %maximum_select_fusion.2), channel_id=1, source_target_pairs={{0,28},{4,0},{8,4},{12,8},{16,12},{20,16},{24,20},{28,24},{1,29},{... | collective-permute-start | bytes 62216 | tf_op jit(solution)/shard_map/while/body/eval_jaxpr/ppermute | solution.py:13
  229.1 9.7 %collective-permute-start.2 = (f32[81,64]{0,1:T(8,128)S(1)}, f32[81,64]{0,1:T(8,128)S(1)}, u32[]{:S(2)}, u32[]{:S(2)}) collective-permute-start(f32[81,64]{0,1:T(8,128)S(1)} %maximum_select_fusion.2), channel_id=1, source_target_pairs={{0,24},{4,28},{8,0},{12,4},{16,8},{20,12},{24,16},{28,20},{1,25},{... | collective-permute-start | bytes 62216 | tf_op jit(solution)/shard_map/while/body/eval_jaxpr/ppermute | solution.py:13
  278.2 14.4 %collective-permute-start.4 = (f32[81,64]{0,1:T(8,128)S(1)}, f32[81,64]{0,1:T(8,128)S(1)}, u32[]{:S(2)}, u32[]{:S(2)}) collective-permute-start(f32[81,64]{0,1:T(8,128)S(1)} %maximum_select_fusion.2), channel_id=1, source_target_pairs={{0,28},{4,0},{8,4},{12,8},{16,12},{20,16},{24,20},{28,24},{1,29},{... | collective-permute-start | bytes 62216 | tf_op jit(solution)/shard_map/while/body/eval_jaxpr/ppermute | solution.py:13
  282.9 9.7 %collective-permute-start.2 = (f32[81,64]{0,1:T(8,128)S(1)}, f32[81,64]{0,1:T(8,128)S(1)}, u32[]{:S(2)}, u32[]{:S(2)}) collective-permute-start(f32[81,64]{0,1:T(8,128)S(1)} %maximum_select_fusion.2), channel_id=1, source_target_pairs={{0,24},{4,28},{8,0},{12,4},{16,8},{20,12},{24,16},{28,20},{1,25},{... | collective-permute-start | bytes 62216 | tf_op jit(solution)/shard_map/while/body/eval_jaxpr/ppermute | solution.py:13
  331.6 14.4 %collective-permute-start.4 = (f32[81,64]{0,1:T(8,128)S(1)}, f32[81,64]{0,1:T(8,128)S(1)}, u32[]{:S(2)}, u32[]{:S(2)}) collective-permute-start(f32[81,64]{0,1:T(8,128)S(1)} %maximum_select_fusion.2), channel_id=1, source_target_pairs={{0,28},{4,0},{8,4},{12,8},{16,12},{20,16},{24,20},{28,24},{1,29},{... | collective-permute-start | bytes 62216 | tf_op jit(solution)/shard_map/while/body/eval_jaxpr/ppermute | solution.py:13
  336.3 9.7 %collective-permute-start.2 = (f32[81,64]{0,1:T(8,128)S(1)}, f32[81,64]{0,1:T(8,128)S(1)}, u32[]{:S(2)}, u32[]{:S(2)}) collective-permute-start(f32[81,64]{0,1:T(8,128)S(1)} %maximum_select_fusion.2), channel_id=1, source_target_pairs={{0,24},{4,28},{8,0},{12,4},{16,8},{20,12},{24,16},{28,20},{1,25},{... | collective-permute-start | bytes 62216 | tf_op jit(solution)/shard_map/while/body/eval_jaxpr/ppermute | solution.py:13
  385.4 14.4 %collective-permute-start.4 = (f32[81,64]{0,1:T(8,128)S(1)}, f32[81,64]{0,1:T(8,128)S(1)}, u32[]{:S(2)}, u32[]{:S(2)}) collective-permute-start(f32[81,64]{0,1:T(8,128)S(1)} %maximum_select_fusion.2), channel_id=1, source_target_pairs={{0,28},{4,0},{8,4},{12,8},{16,12},{20,16},{24,20},{28,24},{1,29},{... | collective-permute-start | bytes 62216 | tf_op jit(solution)/shard_map/while/body/eval_jaxpr/ppermute | solution.py:13
  390.1 9.7 %collective-permute-start.2 = (f32[81,64]{0,1:T(8,128)S(1)}, f32[81,64]{0,1:T(8,128)S(1)}, u32[]{:S(2)}, u32[]{:S(2)}) collective-permute-start(f32[81,64]{0,1:T(8,128)S(1)} %maximum_select_fusion.2), channel_id=1, source_target_pairs={{0,24},{4,28},{8,0},{12,4},{16,8},{20,12},{24,16},{28,20},{1,25},{... | collective-permute-start | bytes 62216 | tf_op jit(solution)/shard_map/while/body/eval_jaxpr/ppermute | solution.py:13
  438.7 14.4 %collective-permute-start.4 = (f32[81,64]{0,1:T(8,128)S(1)}, f32[81,64]{0,1:T(8,128)S(1)}, u32[]{:S(2)}, u32[]{:S(2)}) collective-permute-start(f32[81,64]{0,1:T(8,128)S(1)} %maximum_select_fusion.2), channel_id=1, source_target_pairs={{0,28},{4,0},{8,4},{12,8},{16,12},{20,16},{24,20},{28,24},{1,29},{... | collective-permute-start | bytes 62216 | tf_op jit(solution)/shard_map/while/body/eval_jaxpr/ppermute | solution.py:13
  443.4 9.7 %collective-permute-start.2 = (f32[81,64]{0,1:T(8,128)S(1)}, f32[81,64]{0,1:T(8,128)S(1)}, u32[]{:S(2)}, u32[]{:S(2)}) collective-permute-start(f32[81,64]{0,1:T(8,128)S(1)} %maximum_select_fusion.2), channel_id=1, source_target_pairs={{0,24},{4,28},{8,0},{12,4},{16,8},{20,12},{24,16},{28,20},{1,25},{... | collective-permute-start | bytes 62216 | tf_op jit(solution)/shard_map/while/body/eval_jaxpr/ppermute | solution.py:13
  492.5 14.4 %collective-permute-start.4 = (f32[81,64]{0,1:T(8,128)S(1)}, f32[81,64]{0,1:T(8,128)S(1)}, u32[]{:S(2)}, u32[]{:S(2)}) collective-permute-start(f32[81,64]{0,1:T(8,128)S(1)} %maximum_select_fusion.2), channel_id=1, source_target_pairs={{0,28},{4,0},{8,4},{12,8},{16,12},{20,16},{24,20},{28,24},{1,29},{... | collective-permute-start | bytes 62216 | tf_op jit(solution)/shard_map/while/body/eval_jaxpr/ppermute | solution.py:13
  497.2 9.7 %collective-permute-start.2 = (f32[81,64]{0,1:T(8,128)S(1)}, f32[81,64]{0,1:T(8,128)S(1)}, u32[]{:S(2)}, u32[]{:S(2)}) collective-permute-start(f32[81,64]{0,1:T(8,128)S(1)} %maximum_select_fusion.2), channel_id=1, source_target_pairs={{0,24},{4,28},{8,0},{12,4},{16,8},{20,12},{24,16},{28,20},{1,25},{... | collective-permute-start | bytes 62216 | tf_op jit(solution)/shard_map/while/body/eval_jaxpr/ppermute | solution.py:13
  545.9 14.4 %collective-permute-start.4 = (f32[81,64]{0,1:T(8,128)S(1)}, f32[81,64]{0,1:T(8,128)S(1)}, u32[]{:S(2)}, u32[]{:S(2)}) collective-permute-start(f32[81,64]{0,1:T(8,128)S(1)} %maximum_select_fusion.2), channel_id=1, source_target_pairs={{0,28},{4,0},{8,4},{12,8},{16,12},{20,16},{24,20},{28,24},{1,29},{... | collective-permute-start | bytes 62216 | tf_op jit(solution)/shard_map/while/body/eval_jaxpr/ppermute | solution.py:13
  550.6 9.7 %collective-permute-start.2 = (f32[81,64]{0,1:T(8,128)S(1)}, f32[81,64]{0,1:T(8,128)S(1)}, u32[]{:S(2)}, u32[]{:S(2)}) collective-permute-start(f32[81,64]{0,1:T(8,128)S(1)} %maximum_select_fusion.2), channel_id=1, source_target_pairs={{0,24},{4,28},{8,0},{12,4},{16,8},{20,12},{24,16},{28,20},{1,25},{... | collective-permute-start | bytes 62216 | tf_op jit(solution)/shard_map/while/body/eval_jaxpr/ppermute | solution.py:13
  599.7 14.4 %collective-permute-start.4 = (f32[81,64]{0,1:T(8,128)S(1)}, f32[81,64]{0,1:T(8,128)S(1)}, u32[]{:S(2)}, u32[]{:S(2)}) collective-permute-start(f32[81,64]{0,1:T(8,128)S(1)} %maximum_select_fusion.2), channel_id=1, source_target_pairs={{0,28},{4,0},{8,4},{12,8},{16,12},{20,16},{24,20},{28,24},{1,29},{... | collective-permute-start | bytes 62216 | tf_op jit(solution)/shard_map/while/body/eval_jaxpr/ppermute | solution.py:13
  604.4 9.7 %collective-permute-start.2 = (f32[81,64]{0,1:T(8,128)S(1)}, f32[81,64]{0,1:T(8,128)S(1)}, u32[]{:S(2)}, u32[]{:S(2)}) collective-permute-start(f32[81,64]{0,1:T(8,128)S(1)} %maximum_select_fusion.2), channel_id=1, source_target_pairs={{0,24},{4,28},{8,0},{12,4},{16,8},{20,12},{24,16},{28,20},{1,25},{... | collective-permute-start | bytes 62216 | tf_op jit(solution)/shard_map/while/body/eval_jaxpr/ppermute | solution.py:13
  653.0 14.4 %collective-permute-start.4 = (f32[81,64]{0,1:T(8,128)S(1)}, f32[81,64]{0,1:T(8,128)S(1)}, u32[]{:S(2)}, u32[]{:S(2)}) collective-permute-start(f32[81,64]{0,1:T(8,128)S(1)} %maximum_select_fusion.2), channel_id=1, source_target_pairs={{0,28},{4,0},{8,4},{12,8},{16,12},{20,16},{24,20},{28,24},{1,29},{... | collective-permute-start | bytes 62216 | tf_op jit(solution)/shard_map/while/body/eval_jaxpr/ppermute | solution.py:13
  657.7 9.7 %collective-permute-start.2 = (f32[81,64]{0,1:T(8,128)S(1)}, f32[81,64]{0,1:T(8,128)S(1)}, u32[]{:S(2)}, u32[]{:S(2)}) collective-permute-start(f32[81,64]{0,1:T(8,128)S(1)} %maximum_select_fusion.2), channel_id=1, source_target_pairs={{0,24},{4,28},{8,0},{12,4},{16,8},{20,12},{24,16},{28,20},{1,25},{... | collective-permute-start | bytes 62216 | tf_op jit(solution)/shard_map/while/body/eval_jaxpr/ppermute | solution.py:13
  706.8 14.4 %collective-permute-start.4 = (f32[81,64]{0,1:T(8,128)S(1)}, f32[81,64]{0,1:T(8,128)S(1)}, u32[]{:S(2)}, u32[]{:S(2)}) collective-permute-start(f32[81,64]{0,1:T(8,128)S(1)} %maximum_select_fusion.2), channel_id=1, source_target_pairs={{0,28},{4,0},{8,4},{12,8},{16,12},{20,16},{24,20},{28,24},{1,29},{... | collective-permute-start | bytes 62216 | tf_op jit(solution)/shard_map/while/body/eval_jaxpr/ppermute | solution.py:13
  754.8 11.7 %collective-permute-start.5 = (f32[81,64]{0,1:T(8,128)S(1)}, f32[81,64]{0,1:T(8,128)S(1)}, u32[]{:S(2)}, u32[]{:S(2)}) collective-permute-start(f32[81,64]{0,1:T(8,128)S(1)} %maximum_select_fusion.2), channel_id=1, source_target_pairs={{0,4},{4,8},{8,12},{12,16},{16,20},{20,24},{24,28},{28,0},{1,5},{5... | collective-permute-start | bytes 62216 | tf_op jit(solution)/shard_map/while/body/eval_jaxpr/ppermute | solution.py:13
  759.3 12.0 %collective-permute-start.4 = (f32[81,64]{0,1:T(8,128)S(1)}, f32[81,64]{0,1:T(8,128)S(1)}, u32[]{:S(2)}, u32[]{:S(2)}) collective-permute-start(f32[81,64]{0,1:T(8,128)S(1)} %maximum_select_fusion.2), channel_id=1, source_target_pairs={{0,28},{4,0},{8,4},{12,8},{16,12},{20,16},{24,20},{28,24},{1,29},{... | collective-permute-start | bytes 62216 | tf_op jit(solution)/shard_map/while/body/eval_jaxpr/ppermute | solution.py:13
  813.1 12.4 %collective-permute-start.4 = (f32[81,64]{0,1:T(8,128)S(1)}, f32[81,64]{0,1:T(8,128)S(1)}, u32[]{:S(2)}, u32[]{:S(2)}) collective-permute-start(f32[81,64]{0,1:T(8,128)S(1)} %maximum_select_fusion.2), channel_id=1, source_target_pairs={{0,28},{4,0},{8,4},{12,8},{16,12},{20,16},{24,20},{28,24},{1,29},{... | collective-permute-start | bytes 62216 | tf_op jit(solution)/shard_map/while/body/eval_jaxpr/ppermute | solution.py:13
  815.8 9.7 %collective-permute-start.2 = (f32[81,64]{0,1:T(8,128)S(1)}, f32[81,64]{0,1:T(8,128)S(1)}, u32[]{:S(2)}, u32[]{:S(2)}) collective-permute-start(f32[81,64]{0,1:T(8,128)S(1)} %maximum_select_fusion.2), channel_id=1, source_target_pairs={{0,24},{4,28},{8,0},{12,4},{16,8},{20,12},{24,16},{28,20},{1,25},{... | collective-permute-start | bytes 62216 | tf_op jit(solution)/shard_map/while/body/eval_jaxpr/ppermute | solution.py:13
  (81 other events, 823.9 us)
where the time goes:
time: 862 us; the launch traced here: 857 us
  blocking collectives  365 us (42%)
  starting transfers between devices  204 us (24%)
  local copies, waits for them, and re-layouts  113 us (13%)
  matrix products  94.3 us (11%)
  loops' own time  70.2 us (8%)
  other arithmetic  8.9 us (1%)
    ppermute x96, starting transfers between devices, shifted(): return lax.ppermute(value, axis, pairs)  204 us
    while x16, blocking collectives  102 us
    dot_general x60, matrix products, product(): jnp.dot(left_side, right_side, precision=lax.Precision.HIGHEST, preferred...  94.3 us
    all_gather x16, blocking collectives, assimilate(): lax.all_gather(innovation, 'gy', axis=0, tiled=True)  90.1 us
    all_gather x16, blocking collectives, assimilate(): lax.all_gather(weighted, 'gy', axis=1, tiled=True)  86.7 us
    all_gather x16, blocking collectives, assimilate(): lax.all_gather(picked, 'gy', axis=1, tiled=True)  86.4 us
    another operation x1, loops' own time, local(): lax.fori_loop(0, BATCHES, assimilate, (start_rows, start_mean))  60.8 us
    while x128, local copies, waits for them, and re-layouts  22.2 us
  transfers between devices with their start and end apart: 96, of which 4 were waited for; matrix products, arithmetic and copies ran while one was open for 1% of the time, Pallas kernels for 0%

commit v1 on v0

--- a/solution.py
+++ b/solution.py
@@ -5,6 +5,18 @@
 
 BATCHES = 16
 REACH = 3
+
+
+def doubled_up(array, axis, dim):
+    ways, here = (lax.axis_size(axis), lax.axis_index(axis))
+    grown, reach = (array, 1)
+    while reach < ways:
+        theirs = lax.ppermute(grown, axis, [(d, d ^ reach) for d in range(ways)])
+        mine_first = jnp.concatenate([grown, theirs], axis=dim)
+        theirs_first = jnp.concatenate([theirs, grown], axis=dim)
+        grown = jnp.where(here & reach == 0, mine_first, theirs_first)
+        reach = 2 * reach
+    return grown
 
 
 def shifted(value, axis, steps):
@@ -66,7 +78,7 @@
         weighted = product(prior_all, root_rows.T)
         gain_part = product(gain_rows, innov_all)
         weighted_all, gain_all = (
-            lax.all_gather(weighted, "gy", axis=1, tiled=True),
+            doubled_up(weighted, "gy", 1),
             lax.all_gather(gain_part, "gy", axis=0, tiled=True),
         )
         obs_lon = root_slab * lon_dev + cells_of // (lat_dev * levels)

time: 862 us -> 815 us (0.945)
  blocking collectives: 365 us -> 291 us
  starting transfers between devices: 204 us -> 218 us
  loops' own time: 70.2 us -> 79.9 us
    all_gather x16 -> x0, blocking collectives: 86.7 us -> none  [assimilate(): lax.all_gather(weighted, 'gy', axis=1, tiled=True)]
    all_gather x16, blocking collectives: 90.1 us -> 114 us  [assimilate(): lax.all_gather(innovation, 'gy', axis=0, tiled=True)]
    ppermute x0 -> x32, starting transfers between devices: none -> 14 us  [doubled_up(): theirs = lax.ppermute(grown, axis, [(d, d ^ reach) for d in range(ways)])]
    while x16, blocking collectives: 102 us -> 90.1 us
  transfers between devices with their start and end apart: 96 -> 128, of which waited for: 4 -> 2; matrix products, arithmetic and copies ran while one was open for 1% -> 5% of each run, Pallas kernels for 0% -> 0%
where the time goes in v1:
time: 815 us; the launch traced here: 811 us
  blocking collectives  291 us (36%)
  starting transfers between devices  218 us (27%)
  local copies, waits for them, and re-layouts  117 us (14%)
  matrix products  94.3 us (12%)
  loops' own time  79.9 us (10%)
  other arithmetic  9.55 us (1%)
    ppermute x96, starting transfers between devices, shifted(): return lax.ppermute(value, axis, pairs)  204 us
    all_gather x16, blocking collectives, assimilate(): lax.all_gather(innovation, 'gy', axis=0, tiled=True)  114 us
    dot_general x60, matrix products, product(): jnp.dot(left_side, right_side, precision=lax.Precision.HIGHEST, preferred...  94.3 us
    while x16, blocking collectives  90.1 us
    all_gather x16, blocking collectives, assimilate(): lax.all_gather(picked, 'gy', axis=1, tiled=True)  86.7 us
    another operation x1, loops' own time, local(): lax.fori_loop(0, BATCHES, assimilate, (start_rows, start_mean))  69.1 us
    while x128, local copies, waits for them, and re-layouts  23.1 us
    dynamic_slice x16, local copies, waits for them, and re-layouts, assimilate(): root_slab = owner[batch_id]  21.2 us
  transfers between devices with their start and end apart: 128, of which 2 were waited for; matrix products, arithmetic and copies ran while one was open for 5% of the time, Pallas kernels for 0%

profile of v1, /device:TPU:0, one launch (start us, length us, event | category | flops | bytes accessed | tf_op | source)
XLA Modules:
  0.0 810.5 jit_solution(12496090137538716553)
XLA Ops:
  3.4 806.1 %while.19 = (s32[]{:T(128)}, f32[80,2048]{1,0:T(8,128)S(1)}, f32[2048]{0:T(1024)S(1)}, s32[16]{0:T(128)}, s32[16]{0:T(128)}, /*index=5*/s32[]{:T(128)}, s32[16,2...) while((s32[]{:T(128)}, f32[80,2048]{1,0:T(8,128)S(1)}, ...), condition=%wide.region_3.4_spmd.clone, body=%wide.region_0.3_spmd.clone.sunk | while | flops 1037648064 | bytes 11454532 | solution.py:110
  35.4 7.0 all-reduce.6
  44.1 5.6 all-reduce.7
  86.0 7.1 all-reduce.6
  94.8 5.6 all-reduce.7
  133.4 7.1 all-reduce.6
  142.2 5.6 all-reduce.7
  184.1 7.1 all-reduce.6
  192.9 5.6 all-reduce.7
  234.8 7.1 all-reduce.6
  243.7 5.6 all-reduce.7
  285.6 7.1 all-reduce.6
  294.4 5.6 all-reduce.7
  336.3 7.1 all-reduce.6
  345.1 5.6 all-reduce.7
  387.0 7.1 all-reduce.6
  395.8 5.6 all-reduce.7
  437.7 7.1 all-reduce.6
  446.6 5.6 all-reduce.7
  488.5 7.1 all-reduce.6
  497.3 5.6 all-reduce.7
  539.2 7.1 all-reduce.6
  548.0 5.6 all-reduce.7
  589.9 7.1 all-reduce.6
  598.7 5.6 all-reduce.7
  640.6 7.1 all-reduce.6
  649.5 5.6 all-reduce.7
  691.4 7.1 all-reduce.6
  738.7 7.1 all-reduce.6
  747.5 5.6 all-reduce.7
  789.4 7.1 all-reduce.6
  798.3 5.6 all-reduce.7
  (1027 shorter events, 609.9 us)
Async XLA Ops:
  12.0 9.9 %collective-permute-start.5 = (f32[81,64]{0,1:T(8,128)S(1)}, f32[81,64]{0,1:T(8,128)S(1)}, u32[]{:S(2)}, u32[]{:S(2)}) collective-permute-start(f32[81,64]{0,1:T(8,128)S(1)} %maximum_select_fusion.4), channel_id=1, source_target_pairs={{0,4},{4,8},{8,12},{12,16},{16,20},{20,24},{24,28},{28,0},{1,5},{5... | collective-permute-start | bytes 62216 | tf_op jit(solution)/shard_map/while/body/eval_jaxpr/ppermute | solution.py:25
  15.0 13.0 %collective-permute-start.4 = (f32[81,64]{0,1:T(8,128)S(1)}, f32[81,64]{0,1:T(8,128)S(1)}, u32[]{:S(2)}, u32[]{:S(2)}) collective-permute-start(f32[81,64]{0,1:T(8,128)S(1)} %maximum_select_fusion.4), channel_id=1, source_target_pairs={{0,28},{4,0},{8,4},{12,8},{16,12},{20,16},{24,20},{28,24},{1,29},{... | collective-permute-start | bytes 62216 | tf_op jit(solution)/shard_map/while/body/eval_jaxpr/ppermute | solution.py:25
  18.1 9.9 %collective-permute-start.2 = (f32[81,64]{0,1:T(8,128)S(1)}, f32[81,64]{0,1:T(8,128)S(1)}, u32[]{:S(2)}, u32[]{:S(2)}) collective-permute-start(f32[81,64]{0,1:T(8,128)S(1)} %maximum_select_fusion.4), channel_id=1, source_target_pairs={{0,24},{4,28},{8,0},{12,4},{16,8},{20,12},{24,16},{28,20},{1,25},{... | collective-permute-start | bytes 62216 | tf_op jit(solution)/shard_map/while/body/eval_jaxpr/ppermute | solution.py:25
  64.2 14.4 %collective-permute-start.4 = (f32[81,64]{0,1:T(8,128)S(1)}, f32[81,64]{0,1:T(8,128)S(1)}, u32[]{:S(2)}, u32[]{:S(2)}) collective-permute-start(f32[81,64]{0,1:T(8,128)S(1)} %maximum_select_fusion.4), channel_id=1, source_target_pairs={{0,28},{4,0},{8,4},{12,8},{16,12},{20,16},{24,20},{28,24},{1,29},{... | collective-permute-start | bytes 62216 | tf_op jit(solution)/shard_map/while/body/eval_jaxpr/ppermute | solution.py:25
  68.7 9.9 %collective-permute-start.2 = (f32[81,64]{0,1:T(8,128)S(1)}, f32[81,64]{0,1:T(8,128)S(1)}, u32[]{:S(2)}, u32[]{:S(2)}) collective-permute-start(f32[81,64]{0,1:T(8,128)S(1)} %maximum_select_fusion.4), channel_id=1, source_target_pairs={{0,24},{4,28},{8,0},{12,4},{16,8},{20,12},{24,16},{28,20},{1,25},{... | collective-permute-start | bytes 62216 | tf_op jit(solution)/shard_map/while/body/eval_jaxpr/ppermute | solution.py:25
  109.1 11.7 %collective-permute-start.5 = (f32[81,64]{0,1:T(8,128)S(1)}, f32[81,64]{0,1:T(8,128)S(1)}, u32[]{:S(2)}, u32[]{:S(2)}) collective-permute-start(f32[81,64]{0,1:T(8,128)S(1)} %maximum_select_fusion.4), channel_id=1, source_target_pairs={{0,4},{4,8},{8,12},{12,16},{16,20},{20,24},{24,28},{28,0},{1,5},{5... | collective-permute-start | bytes 62216 | tf_op jit(solution)/shard_map/while/body/eval_jaxpr/ppermute | solution.py:25
  113.7 12.1 %collective-permute-start.4 = (f32[81,64]{0,1:T(8,128)S(1)}, f32[81,64]{0,1:T(8,128)S(1)}, u32[]{:S(2)}, u32[]{:S(2)}) collective-permute-start(f32[81,64]{0,1:T(8,128)S(1)} %maximum_select_fusion.4), channel_id=1, source_target_pairs={{0,28},{4,0},{8,4},{12,8},{16,12},{20,16},{24,20},{28,24},{1,29},{... | collective-permute-start | bytes 62216 | tf_op jit(solution)/shard_map/while/body/eval_jaxpr/ppermute | solution.py:25
  164.1 12.6 %collective-permute-start.4 = (f32[81,64]{0,1:T(8,128)S(1)}, f32[81,64]{0,1:T(8,128)S(1)}, u32[]{:S(2)}, u32[]{:S(2)}) collective-permute-start(f32[81,64]{0,1:T(8,128)S(1)} %maximum_select_fusion.4), channel_id=1, source_target_pairs={{0,28},{4,0},{8,4},{12,8},{16,12},{20,16},{24,20},{28,24},{1,29},{... | collective-permute-start | bytes 62216 | tf_op jit(solution)/shard_map/while/body/eval_jaxpr/ppermute | solution.py:25
  166.8 9.9 %collective-permute-start.2 = (f32[81,64]{0,1:T(8,128)S(1)}, f32[81,64]{0,1:T(8,128)S(1)}, u32[]{:S(2)}, u32[]{:S(2)}) collective-permute-start(f32[81,64]{0,1:T(8,128)S(1)} %maximum_select_fusion.4), channel_id=1, source_target_pairs={{0,24},{4,28},{8,0},{12,4},{16,8},{20,12},{24,16},{28,20},{1,25},{... | collective-permute-start | bytes 62216 | tf_op jit(solution)/shard_map/while/body/eval_jaxpr/ppermute | solution.py:25
  213.0 14.4 %collective-permute-start.4 = (f32[81,64]{0,1:T(8,128)S(1)}, f32[81,64]{0,1:T(8,128)S(1)}, u32[]{:S(2)}, u32[]{:S(2)}) collective-permute-start(f32[81,64]{0,1:T(8,128)S(1)} %maximum_select_fusion.4), channel_id=1, source_target_pairs={{0,28},{4,0},{8,4},{12,8},{16,12},{20,16},{24,20},{28,24},{1,29},{... | collective-permute-start | bytes 62216 | tf_op jit(solution)/shard_map/while/body/eval_jaxpr/ppermute | solution.py:25
  217.5 9.9 %collective-permute-start.2 = (f32[81,64]{0,1:T(8,128)S(1)}, f32[81,64]{0,1:T(8,128)S(1)}, u32[]{:S(2)}, u32[]{:S(2)}) collective-permute-start(f32[81,64]{0,1:T(8,128)S(1)} %maximum_select_fusion.4), channel_id=1, source_target_pairs={{0,24},{4,28},{8,0},{12,4},{16,8},{20,12},{24,16},{28,20},{1,25},{... | collective-permute-start | bytes 62216 | tf_op jit(solution)/shard_map/while/body/eval_jaxpr/ppermute | solution.py:25
  263.5 14.6 %collective-permute-start.4 = (f32[81,64]{0,1:T(8,128)S(1)}, f32[81,64]{0,1:T(8,128)S(1)}, u32[]{:S(2)}, u32[]{:S(2)}) collective-permute-start(f32[81,64]{0,1:T(8,128)S(1)} %maximum_select_fusion.4), channel_id=1, source_target_pairs={{0,28},{4,0},{8,4},{12,8},{16,12},{20,16},{24,20},{28,24},{1,29},{... | collective-permute-start | bytes 62216 | tf_op jit(solution)/shard_map/while/body/eval_jaxpr/ppermute | solution.py:25
  268.2 9.9 %collective-permute-start.2 = (f32[81,64]{0,1:T(8,128)S(1)}, f32[81,64]{0,1:T(8,128)S(1)}, u32[]{:S(2)}, u32[]{:S(2)}) collective-permute-start(f32[81,64]{0,1:T(8,128)S(1)} %maximum_select_fusion.4), channel_id=1, source_target_pairs={{0,24},{4,28},{8,0},{12,4},{16,8},{20,12},{24,16},{28,20},{1,25},{... | collective-permute-start | bytes 62216 | tf_op jit(solution)/shard_map/while/body/eval_jaxpr/ppermute | solution.py:25
  314.2 14.6 %collective-permute-start.4 = (f32[81,64]{0,1:T(8,128)S(1)}, f32[81,64]{0,1:T(8,128)S(1)}, u32[]{:S(2)}, u32[]{:S(2)}) collective-permute-start(f32[81,64]{0,1:T(8,128)S(1)} %maximum_select_fusion.4), channel_id=1, source_target_pairs={{0,28},{4,0},{8,4},{12,8},{16,12},{20,16},{24,20},{28,24},{1,29},{... | collective-permute-start | bytes 62216 | tf_op jit(solution)/shard_map/while/body/eval_jaxpr/ppermute | solution.py:25
  318.9 9.9 %collective-permute-start.2 = (f32[81,64]{0,1:T(8,128)S(1)}, f32[81,64]{0,1:T(8,128)S(1)}, u32[]{:S(2)}, u32[]{:S(2)}) collective-permute-start(f32[81,64]{0,1:T(8,128)S(1)} %maximum_select_fusion.4), channel_id=1, source_target_pairs={{0,24},{4,28},{8,0},{12,4},{16,8},{20,12},{24,16},{28,20},{1,25},{... | collective-permute-start | bytes 62216 | tf_op jit(solution)/shard_map/while/body/eval_jaxpr/ppermute | solution.py:25
  364.9 14.6 %collective-permute-start.4 = (f32[81,64]{0,1:T(8,128)S(1)}, f32[81,64]{0,1:T(8,128)S(1)}, u32[]{:S(2)}, u32[]{:S(2)}) collective-permute-start(f32[81,64]{0,1:T(8,128)S(1)} %maximum_select_fusion.4), channel_id=1, source_target_pairs={{0,28},{4,0},{8,4},{12,8},{16,12},{20,16},{24,20},{28,24},{1,29},{... | collective-permute-start | bytes 62216 | tf_op jit(solution)/shard_map/while/body/eval_jaxpr/ppermute | solution.py:25
  369.7 9.9 %collective-permute-start.2 = (f32[81,64]{0,1:T(8,128)S(1)}, f32[81,64]{0,1:T(8,128)S(1)}, u32[]{:S(2)}, u32[]{:S(2)}) collective-permute-start(f32[81,64]{0,1:T(8,128)S(1)} %maximum_select_fusion.4), channel_id=1, source_target_pairs={{0,24},{4,28},{8,0},{12,4},{16,8},{20,12},{24,16},{28,20},{1,25},{... | collective-permute-start | bytes 62216 | tf_op jit(solution)/shard_map/while/body/eval_jaxpr/ppermute | solution.py:25
  415.7 14.6 %collective-permute-start.4 = (f32[81,64]{0,1:T(8,128)S(1)}, f32[81,64]{0,1:T(8,128)S(1)}, u32[]{:S(2)}, u32[]{:S(2)}) collective-permute-start(f32[81,64]{0,1:T(8,128)S(1)} %maximum_select_fusion.4), channel_id=1, source_target_pairs={{0,28},{4,0},{8,4},{12,8},{16,12},{20,16},{24,20},{28,24},{1,29},{... | collective-permute-start | bytes 62216 | tf_op jit(solution)/shard_map/while/body/eval_jaxpr/ppermute | solution.py:25
  420.4 9.9 %collective-permute-start.2 = (f32[81,64]{0,1:T(8,128)S(1)}, f32[81,64]{0,1:T(8,128)S(1)}, u32[]{:S(2)}, u32[]{:S(2)}) collective-permute-start(f32[81,64]{0,1:T(8,128)S(1)} %maximum_select_fusion.4), channel_id=1, source_target_pairs={{0,24},{4,28},{8,0},{12,4},{16,8},{20,12},{24,16},{28,20},{1,25},{... | collective-permute-start | bytes 62216 | tf_op jit(solution)/shard_map/while/body/eval_jaxpr/ppermute | solution.py:25
  466.4 14.6 %collective-permute-start.4 = (f32[81,64]{0,1:T(8,128)S(1)}, f32[81,64]{0,1:T(8,128)S(1)}, u32[]{:S(2)}, u32[]{:S(2)}) collective-permute-start(f32[81,64]{0,1:T(8,128)S(1)} %maximum_select_fusion.4), channel_id=1, source_target_pairs={{0,28},{4,0},{8,4},{12,8},{16,12},{20,16},{24,20},{28,24},{1,29},{... | collective-permute-start | bytes 62216 | tf_op jit(solution)/shard_map/while/body/eval_jaxpr/ppermute | solution.py:25
  471.1 9.9 %collective-permute-start.2 = (f32[81,64]{0,1:T(8,128)S(1)}, f32[81,64]{0,1:T(8,128)S(1)}, u32[]{:S(2)}, u32[]{:S(2)}) collective-permute-start(f32[81,64]{0,1:T(8,128)S(1)} %maximum_select_fusion.4), channel_id=1, source_target_pairs={{0,24},{4,28},{8,0},{12,4},{16,8},{20,12},{24,16},{28,20},{1,25},{... | collective-permute-start | bytes 62216 | tf_op jit(solution)/shard_map/while/body/eval_jaxpr/ppermute | solution.py:25
  517.1 14.6 %collective-permute-start.4 = (f32[81,64]{0,1:T(8,128)S(1)}, f32[81,64]{0,1:T(8,128)S(1)}, u32[]{:S(2)}, u32[]{:S(2)}) collective-permute-start(f32[81,64]{0,1:T(8,128)S(1)} %maximum_select_fusion.4), channel_id=1, source_target_pairs={{0,28},{4,0},{8,4},{12,8},{16,12},{20,16},{24,20},{28,24},{1,29},{... | collective-permute-start | bytes 62216 | tf_op jit(solution)/shard_map/while/body/eval_jaxpr/ppermute | solution.py:25
  521.8 9.9 %collective-permute-start.2 = (f32[81,64]{0,1:T(8,128)S(1)}, f32[81,64]{0,1:T(8,128)S(1)}, u32[]{:S(2)}, u32[]{:S(2)}) collective-permute-start(f32[81,64]{0,1:T(8,128)S(1)} %maximum_select_fusion.4), channel_id=1, source_target_pairs={{0,24},{4,28},{8,0},{12,4},{16,8},{20,12},{24,16},{28,20},{1,25},{... | collective-permute-start | bytes 62216 | tf_op jit(solution)/shard_map/while/body/eval_jaxpr/ppermute | solution.py:25
  567.8 14.6 %collective-permute-start.4 = (f32[81,64]{0,1:T(8,128)S(1)}, f32[81,64]{0,1:T(8,128)S(1)}, u32[]{:S(2)}, u32[]{:S(2)}) collective-permute-start(f32[81,64]{0,1:T(8,128)S(1)} %maximum_select_fusion.4), channel_id=1, source_target_pairs={{0,28},{4,0},{8,4},{12,8},{16,12},{20,16},{24,20},{28,24},{1,29},{... | collective-permute-start | bytes 62216 | tf_op jit(solution)/shard_map/while/body/eval_jaxpr/ppermute | solution.py:25
  572.6 9.9 %collective-permute-start.2 = (f32[81,64]{0,1:T(8,128)S(1)}, f32[81,64]{0,1:T(8,128)S(1)}, u32[]{:S(2)}, u32[]{:S(2)}) collective-permute-start(f32[81,64]{0,1:T(8,128)S(1)} %maximum_select_fusion.4), channel_id=1, source_target_pairs={{0,24},{4,28},{8,0},{12,4},{16,8},{20,12},{24,16},{28,20},{1,25},{... | collective-permute-start | bytes 62216 | tf_op jit(solution)/shard_map/while/body/eval_jaxpr/ppermute | solution.py:25
  618.6 14.6 %collective-permute-start.4 = (f32[81,64]{0,1:T(8,128)S(1)}, f32[81,64]{0,1:T(8,128)S(1)}, u32[]{:S(2)}, u32[]{:S(2)}) collective-permute-start(f32[81,64]{0,1:T(8,128)S(1)} %maximum_select_fusion.4), channel_id=1, source_target_pairs={{0,28},{4,0},{8,4},{12,8},{16,12},{20,16},{24,20},{28,24},{1,29},{... | collective-permute-start | bytes 62216 | tf_op jit(solution)/shard_map/while/body/eval_jaxpr/ppermute | solution.py:25
  623.3 9.9 %collective-permute-start.2 = (f32[81,64]{0,1:T(8,128)S(1)}, f32[81,64]{0,1:T(8,128)S(1)}, u32[]{:S(2)}, u32[]{:S(2)}) collective-permute-start(f32[81,64]{0,1:T(8,128)S(1)} %maximum_select_fusion.4), channel_id=1, source_target_pairs={{0,24},{4,28},{8,0},{12,4},{16,8},{20,12},{24,16},{28,20},{1,25},{... | collective-permute-start | bytes 62216 | tf_op jit(solution)/shard_map/while/body/eval_jaxpr/ppermute | solution.py:25
  669.3 14.6 %collective-permute-start.4 = (f32[81,64]{0,1:T(8,128)S(1)}, f32[81,64]{0,1:T(8,128)S(1)}, u32[]{:S(2)}, u32[]{:S(2)}) collective-permute-start(f32[81,64]{0,1:T(8,128)S(1)} %maximum_select_fusion.4), channel_id=1, source_target_pairs={{0,28},{4,0},{8,4},{12,8},{16,12},{20,16},{24,20},{28,24},{1,29},{... | collective-permute-start | bytes 62216 | tf_op jit(solution)/shard_map/while/body/eval_jaxpr/ppermute | solution.py:25
  674.0 9.9 %collective-permute-start.2 = (f32[81,64]{0,1:T(8,128)S(1)}, f32[81,64]{0,1:T(8,128)S(1)}, u32[]{:S(2)}, u32[]{:S(2)}) collective-permute-start(f32[81,64]{0,1:T(8,128)S(1)} %maximum_select_fusion.4), channel_id=1, source_target_pairs={{0,24},{4,28},{8,0},{12,4},{16,8},{20,12},{24,16},{28,20},{1,25},{... | collective-permute-start | bytes 62216 | tf_op jit(solution)/shard_map/while/body/eval_jaxpr/ppermute | solution.py:25
  714.4 11.7 %collective-permute-start.5 = (f32[81,64]{0,1:T(8,128)S(1)}, f32[81,64]{0,1:T(8,128)S(1)}, u32[]{:S(2)}, u32[]{:S(2)}) collective-permute-start(f32[81,64]{0,1:T(8,128)S(1)} %maximum_select_fusion.4), channel_id=1, source_target_pairs={{0,4},{4,8},{8,12},{12,16},{16,20},{20,24},{24,28},{28,0},{1,5},{5... | collective-permute-start | bytes 62216 | tf_op jit(solution)/shard_map/while/body/eval_jaxpr/ppermute | solution.py:25
  719.0 12.1 %collective-permute-start.4 = (f32[81,64]{0,1:T(8,128)S(1)}, f32[81,64]{0,1:T(8,128)S(1)}, u32[]{:S(2)}, u32[]{:S(2)}) collective-permute-start(f32[81,64]{0,1:T(8,128)S(1)} %maximum_select_fusion.4), channel_id=1, source_target_pairs={{0,28},{4,0},{8,4},{12,8},{16,12},{20,16},{24,20},{28,24},{1,29},{... | collective-permute-start | bytes 62216 | tf_op jit(solution)/shard_map/while/body/eval_jaxpr/ppermute | solution.py:25
  769.4 12.6 %collective-permute-start.4 = (f32[81,64]{0,1:T(8,128)S(1)}, f32[81,64]{0,1:T(8,128)S(1)}, u32[]{:S(2)}, u32[]{:S(2)}) collective-permute-start(f32[81,64]{0,1:T(8,128)S(1)} %maximum_select_fusion.4), channel_id=1, source_target_pairs={{0,28},{4,0},{8,4},{12,8},{16,12},{20,16},{24,20},{28,24},{1,29},{... | collective-permute-start | bytes 62216 | tf_op jit(solution)/shard_map/while/body/eval_jaxpr/ppermute | solution.py:25
  (113 other events, 1086.0 us)
